TPU v7x, 32 devices: a whole 2x2x4 slice. The times are simulated.
32 devices in a mesh: seq: 8 (over y, x, core), rep: 4 (over z).
Axes of the slice: x: 2, y: 2, z: 4, core: 2. Of those that a mesh axis runs over, the one named last changes fastest.
Arguments:
- query_rows: bfloat16 [8, 8, 256, 1152], P('rep', 'seq'), as said below
- key_rows: bfloat16 [8, 8, 256, 1152], P('rep', 'seq'), as said below
- value_rows: bfloat16 [8, 8, 256, 1152], P('rep', 'seq'), may hold values from -6 to 6
- out_grad: bfloat16 [8, 8, 256, 1152], P('rep', 'seq'), may hold values from -6 to 6
- out_weight: bfloat16 [1152, 1152], replicated, may hold values from -0.1875 to 0.1875
- frame_count: int32 [8], P('rep'), may hold values from 1 to 8, as said below
- pos_count: int32 [8], P('rep'), may hold values from 64 to 256, as said below
Outputs:
- projected: bfloat16 [8, 8, 256, 1152], P('rep', 'seq')
- grad_query: bfloat16 [8, 8, 256, 1152], P('rep', 'seq')
- grad_key: bfloat16 [8, 8, 256, 1152], P('rep', 'seq')
- grad_value: bfloat16 [8, 8, 256, 1152], P('rep', 'seq')
- grad_weight: float32 [1152, 1152], P('seq')
Inputs may be any that keep to these rules, and one draw needn't show every extreme that they name: `query_rows`: entries lie within -40 to 40. `key_rows`: entries lie within -40 to 40. `frame_count`: some clip has all 8 frames live. `pos_count`: some clip has all 256 positions live.
All inputs are finite; a program needn't handle non-finite values.
Results may differ from a plain program's by a relative error of at most 0.0057.
Values may be sent and summed in bfloat16 or wider, within the bound.
No kernel may reach another device: no remote copies, remote signals or barrier semaphores. Data moves between devices by JAX's collectives and lax.ppermute only.
A program may use at most 128 MiB of HBM per device.

v0:
```python
import math
import jax
import jax.numpy as jnp
from jax import lax
from jax.sharding import PartitionSpec as P

HEADS = 16


def attend_local(query_part, key_part, value_part, key_live, row_live):
    nframe, npos_part, width = query_part.shape
    head_dim = width // HEADS
    inv_root = 1.0 / math.sqrt(head_dim)
    shape_heads = (nframe, npos_part, HEADS, head_dim)
    query_heads = query_part.reshape(shape_heads)
    key_heads = key_part.reshape(shape_heads)
    value_heads = value_part.reshape(shape_heads)
    scores = (
        jnp.einsum("fphd,tphd->phft", query_heads, key_heads, preferred_element_type=jnp.float32)
        * inv_root
    )
    scores = jnp.where(key_live, scores, -1e30)
    highest = jnp.max(scores, axis=-1, keepdims=True)
    expo = jnp.exp(scores - highest) * key_live.astype(jnp.float32)
    weights = expo / jnp.sum(expo, axis=-1, keepdims=True)
    rounded = weights.astype(jnp.bfloat16)
    mixed = jnp.einsum("phft,tphd->fphd", rounded, value_heads, preferred_element_type=jnp.float32)
    attn_out = jnp.where(row_live[:, :, None], mixed.reshape(nframe, npos_part, width), 0.0).astype(
        jnp.bfloat16
    )
    return (attn_out, weights, rounded)


def attend_back(query_part, key_part, value_part, cot_part, weights, rounded):
    nframe, npos_part, width = query_part.shape
    head_dim = width // HEADS
    inv_root = 1.0 / math.sqrt(head_dim)
    shape_heads = (nframe, npos_part, HEADS, head_dim)
    cot_heads = cot_part.reshape(shape_heads)
    value_heads = value_part.reshape(shape_heads)
    grad_value = jnp.einsum(
        "phft,fphd->tphd", rounded, cot_heads, preferred_element_type=jnp.float32
    )
    grad_attn = jnp.einsum(
        "fphd,tphd->phft", cot_heads, value_heads, preferred_element_type=jnp.float32
    )
    row_delta = jnp.sum(weights * grad_attn, axis=-1, keepdims=True)
    grad_score = weights * (grad_attn - row_delta) * inv_root
    key_wide = key_part.astype(jnp.float32).reshape(shape_heads)
    query_wide = query_part.astype(jnp.float32).reshape(shape_heads)
    grad_query = jnp.einsum(
        "phft,tphd->fphd", grad_score, key_wide, precision=lax.Precision.HIGHEST
    )
    grad_key = jnp.einsum(
        "phft,fphd->tphd", grad_score, query_wide, precision=lax.Precision.HIGHEST
    )
    full = (nframe, npos_part, width)
    return (
        grad_query.reshape(full).astype(jnp.bfloat16),
        grad_key.reshape(full).astype(jnp.bfloat16),
        grad_value.reshape(full).astype(jnp.bfloat16),
    )


def reduce_weight(flat_grad, flat_out):
    mine = lax.psum_scatter(
        lax.dot_general(
            flat_grad, flat_out, (((0,), (0,)), ((), ())), preferred_element_type=jnp.float32
        ),
        "seq",
        scatter_dimension=0,
        tiled=True,
    )
    return lax.psum(mine, "rep")


def shards(query_rows, key_rows, value_rows, out_grad, out_weight, frame_count, pos_count):
    clip_local, frame_local, npos_all, width = query_rows.shape
    rank = lax.axis_index("seq")
    query_pos, key_pos, value_pos = (
        lax.all_to_all(query_rows, "seq", split_axis=2, concat_axis=1, tiled=True),
        lax.all_to_all(key_rows, "seq", split_axis=2, concat_axis=1, tiled=True),
        lax.all_to_all(value_rows, "seq", split_axis=2, concat_axis=1, tiled=True),
    )
    nframe = query_pos.shape[1]
    npos_part = query_pos.shape[2]
    frame_ids = jnp.arange(nframe, dtype=jnp.int32)
    position_ids = rank * npos_part + jnp.arange(npos_part, dtype=jnp.int32)
    key_live = frame_ids[None, :] < frame_count[:, None]
    row_live = key_live[:, :, None] & (position_ids[None, None, :] < pos_count[:, None, None])
    attn_pos, weights, rounded = jax.vmap(attend_local)(
        query_pos, key_pos, value_pos, key_live, row_live
    )
    attn_frames = lax.all_to_all(attn_pos, "seq", split_axis=1, concat_axis=2, tiled=True)
    flat_out = attn_frames.reshape(-1, width)
    flat_grad = out_grad.reshape(-1, width)
    projected = lax.dot_general(
        flat_out, out_weight, (((1,), (1,)), ((), ())), preferred_element_type=jnp.float32
    )
    projected = projected.astype(jnp.bfloat16).reshape(query_rows.shape)
    own_frames = rank * frame_local + jnp.arange(frame_local, dtype=jnp.int32)
    frame_alive = own_frames[None, :, None] < frame_count[:, None, None]
    place_alive = jnp.arange(npos_all, dtype=jnp.int32)[None, None, :] < pos_count[:, None, None]
    out_cot = jnp.dot(flat_grad, out_weight, preferred_element_type=jnp.float32).reshape(
        query_rows.shape
    )
    out_cot = jnp.where((frame_alive & place_alive)[..., None], out_cot, 0.0).astype(jnp.bfloat16)
    cot_pos = lax.all_to_all(out_cot, "seq", split_axis=2, concat_axis=1, tiled=True)
    grad_query_pos, grad_key_pos, grad_value_pos = jax.vmap(attend_back)(
        query_pos, key_pos, value_pos, cot_pos, weights, rounded
    )
    grad_query, grad_key, grad_value = (
        lax.all_to_all(grad_query_pos, "seq", split_axis=1, concat_axis=2, tiled=True),
        lax.all_to_all(grad_key_pos, "seq", split_axis=1, concat_axis=2, tiled=True),
        lax.all_to_all(grad_value_pos, "seq", split_axis=1, concat_axis=2, tiled=True),
    )
    grad_weight = reduce_weight(flat_grad, flat_out)
    return (projected, grad_query, grad_key, grad_value, grad_weight)


def solution(mesh):
    in_specs = (
        P("rep", "seq", None, None),
        P("rep", "seq", None, None),
        P("rep", "seq", None, None),
        P("rep", "seq", None, None),
        P(),
        P("rep"),
        P("rep"),
    )
    out_specs = (
        P("rep", "seq", None, None),
        P("rep", "seq", None, None),
        P("rep", "seq", None, None),
        P("rep", "seq", None, None),
        P("seq", None),
    )
    return jax.shard_map(shards, mesh=mesh, in_specs=in_specs, out_specs=out_specs, check_vma=False)
```

profile of v0, /device:TPU:0, one launch (start us, length us, event | category | flops | bytes accessed | tf_op | source)
XLA Modules:
  0.0 298.1 jit_solution(12987899901119479207)
XLA Ops:
  7.2 0.0 copy-start
  7.2 3.6 %copy.97 = bf16[2,1,256,1152]{3,0,1,2:T(2,128)(2,1)} copy(bf16[2,1,256,1152]{3,2,1,0:T(8,128)(2,1)} %param.7) | data formatting | bytes 2359296 | tf_op args[0]
  10.8 5.2 %all-to-all-start = ((bf16[2,1,256,1152]{3,0,1,2:T(2,128)(2,1)}), bf16[2,1,256,1152]{3,0,1,2:T(2,128)(2,1)}, u32[]{:S(2)}, u32[]{:S(2)}) async-start(bf16[2,1,256,1152]{3,0,1,2:T(2,128)(2,1)} %copy.97), calls=%async_computation | async-start | bytes 2359296 | tf_op jit(solution)/shard_map/all_to_all | solution.py:81
  16.0 3.5 %copy.99 = bf16[2,1,256,1152]{3,0,1,2:T(2,128)(2,1)} copy(bf16[2,1,256,1152]{3,2,1,0:T(8,128)(2,1)} %param.8) | data formatting | bytes 2359296 | tf_op args[1]
  19.5 13.4 %all-to-all-done = bf16[2,1,256,1152]{3,0,1,2:T(2,128)(2,1)} async-done(((bf16[2,1,256,1152]{3,0,1,2:T(2,128)(2,1)}), bf16[2,1,256,1152]{3,0,1,2:T(2,128)(2,1)}, u32[]{:S(2)}, u32[]{:S(2)}) %all-to-all-start) | async-done | bytes 1179680 | tf_op jit(solution)/shard_map/all_to_all | solution.py:81
  32.9 4.3 %all-to-all-start.1 = ((bf16[2,1,256,1152]{3,0,1,2:T(2,128)(2,1)}), bf16[2,1,256,1152]{3,0,1,2:T(2,128)(2,1)}, u32[]{:S(2)}, u32[]{:S(2)}) async-start(bf16[2,1,256,1152]{3,0,1,2:T(2,128)(2,1)} %copy.99), calls=%async_computation.1 | async-start | bytes 2359296 | tf_op jit(solution)/shard_map/all_to_all | solution.py:82
  37.2 0.0 copy-start.6
  37.2 0.0 copy-start.5
  37.2 3.5 %copy.103 = bf16[2,1,256,1152]{3,0,1,2:T(2,128)(2,1)} copy(bf16[2,1,256,1152]{3,2,1,0:T(8,128)(2,1)} %param.9) | data formatting | bytes 2359296 | tf_op args[2]
  40.7 13.3 %all-to-all-done.1 = bf16[2,1,256,1152]{3,0,1,2:T(2,128)(2,1)} async-done(((bf16[2,1,256,1152]{3,0,1,2:T(2,128)(2,1)}), bf16[2,1,256,1152]{3,0,1,2:T(2,128)(2,1)}, u32[]{:S(2)}, u32[]{:S(2)}) %all-to-all-start.1) | async-done | bytes 1179680 | tf_op jit(solution)/shard_map/all_to_all | solution.py:82
  54.0 4.2 %all-to-all-start.2 = ((bf16[2,1,256,1152]{3,0,1,2:T(2,128)(2,1)}), bf16[2,1,256,1152]{3,0,1,2:T(2,128)(2,1)}, u32[]{:S(2)}, u32[]{:S(2)}) async-start(bf16[2,1,256,1152]{3,0,1,2:T(2,128)(2,1)} %copy.103), calls=%async_computation.2 | async-start | bytes 2359296 | tf_op jit(solution)/shard_map/all_to_all | solution.py:83
  58.2 0.6 reduce-scatter.4.cloned.1.call-start
  58.8 0.1 broadcast_compare_fusion
  58.9 0.1 iota_compare_fusion
  59.0 0.1 broadcast_and_fusion
  59.0 6.5 %reshape.214 = bf16[2,8,32,16,72]{4,3,0,2,1:T(8,128)(2,1)} reshape(bf16[2,1,256,1152]{3,0,1,2:T(2,128)(2,1)} %all-to-all-done) | data formatting | bytes 2359296 | tf_op jit(solution)/shard_map/vmap()/reshape | solution.py:15
  65.6 6.5 %reshape.215 = bf16[2,8,32,16,72]{4,3,0,2,1:T(8,128)(2,1)} reshape(bf16[2,1,256,1152]{3,0,1,2:T(2,128)(2,1)} %all-to-all-done.1) | data formatting | bytes 2359296 | tf_op jit(solution)/shard_map/vmap()/reshape | solution.py:16
  72.1 8.7 %fusion.38 = (f32[2,32,16,8]{3,2,1,0:T(8,128)S(1)}, f32[2,32,16,8,8]{3,4,2,1,0:T(8,128)}) fusion(f32[2,8]{1,0:T(2,128)S(1)} %get-tuple-element.31, pred[2,8]{1,0:T(4,128)(4,1)S(1)} %get-tuple-element.30, bf16[2,8,32,16,72]{4,3,0,2,1:T(8,128)(2,1)} %reshape.215, bf16[2,8,32,16,72]{4,3,0,2,1:T(8,128)(2,1)} %reshape.214), kind=kOutput, calls=%fused_computation.48 | convolution fusion | flops 9764871 | bytes 2654288 | tf_op jit(solution)/shard_map/vmap()/sub | solution.py:24
  80.8 0.0 all-to-all-done.2
  80.8 6.5 %reshape.216 = bf16[2,8,32,16,72]{4,3,0,2,1:T(8,128)(2,1)} reshape(bf16[2,1,256,1152]{3,0,1,2:T(2,128)(2,1)} %all-to-all-done.2) | data formatting | bytes 2359296 | tf_op jit(solution)/shard_map/vmap()/reshape | solution.py:17
  87.3 4.1 %convolution_bitcast_fusion.1 = bf16[2,8,32,16,72]{4,1,3,2,0:T(8,128)(2,1)S(1)} fusion(bf16[2,8,32,16,72]{4,3,0,2,1:T(8,128)(2,1)} %reshape.216, f32[2,32,16,8,8]{3,4,2,1,0:T(8,128)} %get-tuple-element.33, f32[2,32,16,8]{3,2,1,0:T(8,128)S(1)} %get-tuple-element.32), kind=kOutput, calls=%fused_computation.13 | convolution fusion | flops 9568256 | bytes 2654208 | tf_op jit(solution)/shard_map/vmap(phft,tphd->fphd)/dot_general | solution.py:27
  91.4 1.7 copy.107
  93.1 4.6 %reshape.203 = bf16[2,8,32,1152]{3,2,1,0:T(8,128)(2,1)} reshape(bf16[2,8,32,16,72]{4,3,2,1,0:T(8,128)(2,1)} %copy.107) | data formatting | bytes 2359296 | tf_op jit(solution)/shard_map/vmap()/reshape | solution.py:28
  97.7 1.5 select_convert_fusion
  99.2 0.1 copy.108
  99.4 0.0 copy-start.4
  99.4 20.7 %all_to_all.81 = bf16[2,8,32,1152]{3,2,0,1:T(8,128)(2,1)S(1)} all-to-all(bf16[2,8,32,1152]{3,2,0,1:T(8,128)(2,1)S(1)} %copy.108), channel_id=1, replica_groups=mesh['seq'=8,'rep'=4] {'seq'}, dimensions={1} | all-to-all | bytes 2359296 | tf_op jit(solution)/shard_map/all_to_all | solution.py:94
  120.1 0.1 copy.109
  120.2 0.0 copy-start.1
  120.2 1.0 copy-done.1
  121.2 4.1 %convolution_bitcast_fusion = f32[1152,1152]{0,1:T(8,128)} fusion(bf16[512,1152]{1,0:T(8,128)(2,1)S(1)} %bitcast.59, bf16[512,1152]{1,0:T(8,128)(2,1)S(1)} %bitcast.64), kind=kOutput, calls=%fused_computation.1 | convolution fusion | flops 1358954496 | bytes 7667712 | tf_op jit(solution)/shard_map/dot_general | solution.py:67
  125.3 6.9 %copy.137 = f32[1152,1152]{1,0:T(8,128)} copy(f32[1152,1152]{0,1:T(8,128)} %convolution_bitcast_fusion) | data formatting | bytes 10616832
  132.2 0.0 reduce-scatter.4.cloned.1.call-update
  132.2 0.1 compare_and_fusion
  132.3 3.1 %fusion.3 = bf16[2,1,256,1152]{3,2,0,1:T(8,128)(2,1)S(1)} fusion(bf16[1152,1152]{1,0:T(8,128)(2,1)S(1)} %copy-done, bf16[2,1,256,1152]{3,2,1,0:T(8,128)(2,1)} %param.10, pred[2,256]{1,0:T(4,128)(4,1)S(1)} %compare_and_fusion), kind=kOutput, calls=%fused_computation.10 | convolution fusion | flops 1360134144 | bytes 5014016 | tf_op jit(solution)/shard_map/dot_general | solution.py:104
  135.4 1.2 copy.110
  136.7 19.9 %all_to_all.82 = bf16[2,1,256,1152]{3,0,1,2:T(2,128)(2,1)} all-to-all(bf16[2,1,256,1152]{3,0,1,2:T(2,128)(2,1)S(1)} %copy.110), channel_id=1, replica_groups=mesh['seq'=8,'rep'=4] {'seq'}, dimensions={2} | all-to-all | bytes 2359296 | tf_op jit(solution)/shard_map/all_to_all | solution.py:108
  156.5 6.5 %reshape.217 = bf16[2,8,32,16,72]{4,3,0,2,1:T(8,128)(2,1)} reshape(bf16[2,1,256,1152]{3,0,1,2:T(2,128)(2,1)} %all_to_all.82) | data formatting | bytes 2359296 | tf_op jit(solution)/shard_map/vmap()/reshape | solution.py:39
  163.0 4.7 %convert_bitcast_fusion = bf16[2,8,32,16,72]{4,1,3,2,0:T(8,128)(2,1)S(1)} fusion(bf16[2,8,32,16,72]{4,3,0,2,1:T(8,128)(2,1)} %reshape.217, f32[2,32,16,8,8]{3,4,2,1,0:T(8,128)} %get-tuple-element.33, f32[2,32,16,8]{3,2,1,0:T(8,128)S(1)} %get-tuple-element.32), kind=kOutput, calls=%fused_computation.14 | convolution fusion | flops 10158080 | bytes 2654208 | tf_op jit(solution)/shard_map/vmap(phft,fphd->tphd)/dot_general | solution.py:41
  167.8 1.8 copy.136
  169.5 4.6 %reshape.211 = bf16[2,8,32,1152]{3,2,0,1:T(8,128)(2,1)} reshape(bf16[2,8,32,16,72]{4,3,2,0,1:T(8,128)(2,1)} %copy.136) | data formatting | bytes 2359296 | tf_op jit(solution)/shard_map/vmap()/convert_element_type | solution.py:61
  174.2 4.5 %all-to-all-start.7 = ((bf16[2,8,32,1152]{3,2,0,1:T(8,128)(2,1)}), bf16[2,8,32,1152]{3,2,0,1:T(8,128)(2,1)}, u32[]{:S(2)}, u32[]{:S(2)}) async-start(bf16[2,8,32,1152]{3,2,0,1:T(8,128)(2,1)} %reshape.211), calls=%async_computation.7 | async-start | bytes 2359296 | tf_op jit(solution)/shard_map/all_to_all | solution.py:115
  178.6 9.1 %multiply_reduce_fusion = (f32[2,32,16,8]{3,2,1,0:T(8,128)S(1)}, f32[2,32,16,8,8]{3,4,2,1,0:T(8,128)}) fusion(f32[2,32,16,8,8]{3,4,2,1,0:T(8,128)} %get-tuple-element.33, f32[2,32,16,8]{3,2,1,0:T(8,128)S(1)} %get-tuple-element.32, bf16[2,8,32,16,72]{4,3,0,2,1:T(8,128)(2,1)} %reshape.216, bf16[2,8,32,16,72]{4,3,0,2,1:T(8,128)(2,1)} %reshape.217), kind=kOutput, calls=%fused_computation.3 | convolution fusion | flops 9625600 | bytes 2949120 | tf_op jit(solution)/shard_map/vmap(fphd,tphd->phft)/dot_general | solution.py:44
  187.7 7.4 %convert_bitcast_fusion.1 = bf16[2,8,32,16,72]{4,1,3,2,0:T(8,128)(2,1)S(1)} fusion(bf16[2,8,32,16,72]{4,3,0,2,1:T(8,128)(2,1)S(1)} %copy-done.3, f32[2,32,16,8,8]{3,4,2,1,0:T(8,128)} %get-tuple-element.35, f32[2,32,16,8]{3,2,1,0:T(8,128)S(1)} %get-tuple-element.34, f32[2,32,16,8,8]{3,4,2,1,0:T(8,128)S(1)} %copy-done.7, ...), kind=kOutput, calls=%fused_computation.15 | convolution fusion | flops 57475072 | bytes 2949120 | tf_op jit(solution)/shard_map/vmap(phft,fphd->tphd)/dot_general | solution.py:54
  195.2 1.9 copy.135
  197.0 4.6 %reshape.210 = bf16[2,8,32,1152]{3,2,0,1:T(8,128)(2,1)} reshape(bf16[2,8,32,16,72]{4,3,2,0,1:T(8,128)(2,1)} %copy.135) | data formatting | bytes 2359296 | tf_op jit(solution)/shard_map/vmap()/convert_element_type | solution.py:60
  201.6 0.0 all-to-all-done.7
  201.6 4.5 %all-to-all-start.6 = ((bf16[2,8,32,1152]{3,2,0,1:T(8,128)(2,1)}), bf16[2,8,32,1152]{3,2,0,1:T(8,128)(2,1)}, u32[]{:S(2)}, u32[]{:S(2)}) async-start(bf16[2,8,32,1152]{3,2,0,1:T(8,128)(2,1)} %reshape.210), calls=%async_computation.6 | async-start | bytes 2359296 | tf_op jit(solution)/shard_map/all_to_all | solution.py:114
  206.1 8.3 %convert_bitcast_fusion.2 = bf16[2,8,32,16,72]{4,1,3,2,0:T(8,128)(2,1)S(1)} fusion(bf16[2,8,32,16,72]{4,3,0,2,1:T(8,128)(2,1)} %reshape.215, f32[2,32,16,8,8]{3,4,2,1,0:T(8,128)} %get-tuple-element.35, f32[2,32,16,8]{3,2,1,0:T(8,128)} %copy-done.8, f32[2,32,16,8,8]{3,4,2,1,0:T(8,128)} %get-tuple-element.33, f32[2,32,16,8]{3,2,1,0:T(8,128)S(1)} %get-tuple-element.32), kind=kOutput, calls=%fused_computation.16 | convolution fusion | flops 57475072 | bytes 2949120 | tf_op jit(solution)/shard_map/vmap(phft,tphd->fphd)/dot_general | solution.py:51
  214.4 1.8 copy.134
  216.2 4.6 %reshape.209 = bf16[2,8,32,1152]{3,2,0,1:T(8,128)(2,1)} reshape(bf16[2,8,32,16,72]{4,3,2,0,1:T(8,128)(2,1)} %copy.134) | data formatting | bytes 2359296 | tf_op jit(solution)/shard_map/vmap()/convert_element_type | solution.py:59
  220.8 2.2 all-to-all-done.6
  222.9 4.3 %all-to-all-start.5 = ((bf16[2,8,32,1152]{3,2,0,1:T(8,128)(2,1)}), bf16[2,8,32,1152]{3,2,0,1:T(8,128)(2,1)}, u32[]{:S(2)}, u32[]{:S(2)}) async-start(bf16[2,8,32,1152]{3,2,0,1:T(8,128)(2,1)} %reshape.209), calls=%async_computation.5 | async-start | bytes 2359296 | tf_op jit(solution)/shard_map/all_to_all | solution.py:113
  227.2 0.0 all-reduce.2.cloned.1.call-start
  227.3 0.0 reduce-scatter.4.cloned.1.call-done
  227.3 2.5 copy.138
  229.8 0.0 all-reduce.2.cloned.1.call-update
  229.8 2.4 copy.126
  232.2 2.4 copy.122
  234.6 9.5 %all-to-all-done.5 = bf16[2,8,32,1152]{3,2,0,1:T(8,128)(2,1)} async-done(((bf16[2,8,32,1152]{3,2,0,1:T(8,128)(2,1)}), bf16[2,8,32,1152]{3,2,0,1:T(8,128)(2,1)}, u32[]{:S(2)}, u32[]{:S(2)}) %all-to-all-start.5) | async-done | bytes 1179680 | tf_op jit(solution)/shard_map/all_to_all | solution.py:113
  244.0 2.5 copy.118
  246.5 2.9 convolution_convert_fusion
  249.4 39.1 %all-reduce.2.cloned.1.call-done = f32[144,1152]{0,1:T(8,128)} async-done(((f32[144,1152]{0,1:T(8,128)}), f32[144,1152]{0,1:T(8,128)}) %all-reduce.2.cloned.1.call-update) | async-done | bytes 663568 | tf_op jit(solution)/shard_map/psum | solution.py:74
  288.5 2.4 copy.131
  (14 shorter events, 0.0 us)
Async XLA Ops:
  7.2 125.2 %copy-start = (bf16[1152,1152]{1,0:T(8,128)(2,1)S(1)}, bf16[1152,1152]{1,0:T(8,128)(2,1)}, u32[]{:S(2)}) copy-start(bf16[1152,1152]{1,0:T(8,128)(2,1)} %param.11) | copy-start | bytes 7962628
  10.8 22.1 %all-to-all-start = ((bf16[2,1,256,1152]{3,0,1,2:T(2,128)(2,1)}), bf16[2,1,256,1152]{3,0,1,2:T(2,128)(2,1)}, u32[]{:S(2)}, u32[]{:S(2)}) async-start(bf16[2,1,256,1152]{3,0,1,2:T(2,128)(2,1)} %copy.97), calls=%async_computation | async-start | bytes 2359296 | tf_op jit(solution)/shard_map/all_to_all | solution.py:81
  32.9 21.1 %all-to-all-start.1 = ((bf16[2,1,256,1152]{3,0,1,2:T(2,128)(2,1)}), bf16[2,1,256,1152]{3,0,1,2:T(2,128)(2,1)}, u32[]{:S(2)}, u32[]{:S(2)}) async-start(bf16[2,1,256,1152]{3,0,1,2:T(2,128)(2,1)} %copy.99), calls=%async_computation.1 | async-start | bytes 2359296 | tf_op jit(solution)/shard_map/all_to_all | solution.py:82
  37.2 21.6 %copy-start.6 = (s32[2]{0:T(128)S(1)}, s32[2]{0:T(128)}, u32[]{:S(2)}) copy-start(s32[2]{0:T(128)} %param.13) | copy-start | bytes 28
  37.2 21.7 %copy-start.5 = (s32[2]{0:T(128)S(1)}, s32[2]{0:T(128)}, u32[]{:S(2)}) copy-start(s32[2]{0:T(128)} %param.12) | copy-start | bytes 28
  54.0 26.8 %all-to-all-start.2 = ((bf16[2,1,256,1152]{3,0,1,2:T(2,128)(2,1)}), bf16[2,1,256,1152]{3,0,1,2:T(2,128)(2,1)}, u32[]{:S(2)}, u32[]{:S(2)}) async-start(bf16[2,1,256,1152]{3,0,1,2:T(2,128)(2,1)} %copy.103), calls=%async_computation.2 | async-start | bytes 2359296 | tf_op jit(solution)/shard_map/all_to_all | solution.py:83
  58.2 169.0 %reduce-scatter.4.cloned.1.call-start = ((), (), s32[]{:S(2)}) async-start(), calls=%async_computation.10 | async-start | bytes 5971968
  99.4 21.8 %copy-start.4 = (bf16[2,1,256,1152]{3,2,1,0:T(8,128)(2,1)S(1)}, bf16[2,1,256,1152]{3,2,1,0:T(8,128)(2,1)}, u32[]{:S(2)}) copy-start(bf16[2,1,256,1152]{3,2,1,0:T(8,128)(2,1)} %param.10) | copy-start | bytes 3538948
  120.2 1.0 copy-start.1
  174.2 27.5 %all-to-all-start.7 = ((bf16[2,8,32,1152]{3,2,0,1:T(8,128)(2,1)}), bf16[2,8,32,1152]{3,2,0,1:T(8,128)(2,1)}, u32[]{:S(2)}, u32[]{:S(2)}) async-start(bf16[2,8,32,1152]{3,2,0,1:T(8,128)(2,1)} %reshape.211), calls=%async_computation.7 | async-start | bytes 2359296 | tf_op jit(solution)/shard_map/all_to_all | solution.py:115
  178.6 9.1 %copy-start.3 = (bf16[2,8,32,16,72]{4,3,0,2,1:T(8,128)(2,1)S(1)}, bf16[2,8,32,16,72]{4,3,0,2,1:T(8,128)(2,1)}, u32[]{:S(2)}) copy-start(bf16[2,8,32,16,72]{4,3,0,2,1:T(8,128)(2,1)} %reshape.214) | copy-start | bytes 3538948
  178.6 9.1 %copy-start.7 = (f32[2,32,16,8,8]{3,4,2,1,0:T(8,128)S(1)}, f32[2,32,16,8,8]{3,4,2,1,0:T(8,128)}, u32[]{:S(2)}) copy-start(f32[2,32,16,8,8]{3,4,2,1,0:T(8,128)} %get-tuple-element.33) | copy-start | bytes 786436
  187.7 7.4 %copy-start.8 = (f32[2,32,16,8]{3,2,1,0:T(8,128)}, f32[2,32,16,8]{3,2,1,0:T(8,128)S(1)}, u32[]{:S(2)}) copy-start(f32[2,32,16,8]{3,2,1,0:T(8,128)S(1)} %get-tuple-element.34) | copy-start | bytes 98308
  201.6 21.3 %all-to-all-start.6 = ((bf16[2,8,32,1152]{3,2,0,1:T(8,128)(2,1)}), bf16[2,8,32,1152]{3,2,0,1:T(8,128)(2,1)}, u32[]{:S(2)}, u32[]{:S(2)}) async-start(bf16[2,8,32,1152]{3,2,0,1:T(8,128)(2,1)} %reshape.210), calls=%async_computation.6 | async-start | bytes 2359296 | tf_op jit(solution)/shard_map/all_to_all | solution.py:114
  222.9 21.1 %all-to-all-start.5 = ((bf16[2,8,32,1152]{3,2,0,1:T(8,128)(2,1)}), bf16[2,8,32,1152]{3,2,0,1:T(8,128)(2,1)}, u32[]{:S(2)}, u32[]{:S(2)}) async-start(bf16[2,8,32,1152]{3,2,0,1:T(8,128)(2,1)} %reshape.209), calls=%async_computation.5 | async-start | bytes 2359296 | tf_op jit(solution)/shard_map/all_to_all | solution.py:113
  227.2 61.3 %all-reduce.2.cloned.1.call-start = ((), (), s32[]{:S(2)}) async-start(), calls=%async_computation.9 | async-start | bytes 2359296 | tf_op jit(solution)/shard_map/psum | solution.py:74
  244.0 2.5 copy-start.2
Sparse Core Ops, SparseCore 0:
  132.3 65.9 reduce-scatter.3
  230.4 58.0 all-reduce.1
where the time goes:
time: 303 us; the launch traced here: 298 us
  local copies, waits for them, and re-layouts  83.8 us (28%)
  waiting for transfers between devices  77.4 us (26%)
  matrix products  52.4 us (17%)
  blocking collectives  40.6 us (13%)
  starting transfers between devices  27.5 us (9%)
  between operations  14.5 us (5%)
    psum x1, waiting for transfers between devices, reduce_weight(): return lax.psum(mine, 'rep')  39.1 us
    unnamed x24, local copies, waits for them, and re-layouts  23.5 us
    all_to_all x1, blocking collectives, shards(): lax.all_to_all(attn_pos, 'seq', split_axis=1, concat_axis=2, tiled=True)  20.7 us
    all_to_all x1, blocking collectives, shards(): lax.all_to_all(out_cot, 'seq', split_axis=2, concat_axis=1, tiled=True)  19.9 us
    all_to_all x1, waiting for transfers between devices, shards(): lax.all_to_all(query_rows, 'seq', split_axis=2, concat_axis=1, tiled=True)  13.4 us
    all_to_all x1, waiting for transfers between devices, shards(): lax.all_to_all(key_rows, 'seq', split_axis=2, concat_axis=1, tiled=True)  13.3 us
    all_to_all x1, waiting for transfers between devices, shards(): lax.all_to_all(grad_query_pos, 'seq', split_axis=1, concat_axis=2, tiled=...  9.45 us
    dot_general x1, matrix products, attend_back(): jnp.einsum('fphd,tphd->phft', cot_heads, value_heads, preferred_element_t...  9.06 us
  transfers between devices with their start and end apart: 8, of which 5 were waited for; matrix products, arithmetic and copies ran while one was open for 34% of the time, Pallas kernels for 0%

commit v1 on v0

--- a/solution.py
+++ b/solution.py
@@ -5,6 +5,10 @@
 from jax.sharding import PartitionSpec as P
 
 HEADS = 16
+
+
+def cut_the_side(slab_in, mesh_ax):
+    return jnp.sum(lax.all_gather(slab_in, mesh_ax), axis=0)
 
 
 def attend_local(query_part, key_part, value_part, key_live, row_live):
@@ -71,7 +75,7 @@
         scatter_dimension=0,
         tiled=True,
     )
-    return lax.psum(mine, "rep")
+    return cut_the_side(mine, "rep")
 
 
 def shards(query_rows, key_rows, value_rows, out_grad, out_weight, frame_count, pos_count):

time: 303 us -> 286 us (0.944)
  waiting for transfers between devices: 77.4 us -> 60.7 us
  local copies, waits for them, and re-layouts: 83.8 us -> 78.8 us
    psum x1 -> x0, waiting for transfers between devices: 39.1 us -> none  [reduce_weight(): return lax.psum(mine, 'rep')]
    reduce_scatter x0 -> x1, waiting for transfers between devices: none -> 19.8 us  [reduce_weight(): lax.psum_scatter(lax.dot_general(flat_grad, flat_out, (((0,), (0,)), ((),...]
    unnamed x24 -> x22, local copies, waits for them, and re-layouts: 23.5 us -> 18.6 us
  transfers between devices with their start and end apart: 8 -> 8, of which waited for: 5 -> 5; matrix products, arithmetic and copies ran while one was open for 34% -> 35% of each run, Pallas kernels for 0% -> 0%
where the time goes in v1:
time: 286 us; the launch traced here: 281 us
  local copies, waits for them, and re-layouts  78.8 us (28%)
  waiting for transfers between devices  60.7 us (21%)
  matrix products  52.6 us (18%)
  blocking collectives  40.6 us (14%)
  starting transfers between devices  29.3 us (10%)
  between operations  14.5 us (5%)
  other arithmetic  4.65 us (2%)
    all_to_all x1, blocking collectives, shards(): lax.all_to_all(attn_pos, 'seq', split_axis=1, concat_axis=2, tiled=True)  20.7 us
    all_to_all x1, blocking collectives, shards(): lax.all_to_all(out_cot, 'seq', split_axis=2, concat_axis=1, tiled=True)  19.9 us
    reduce_scatter x1, waiting for transfers between devices, reduce_weight(): lax.psum_scatter(lax.dot_general(flat_grad, flat_out, (((0,), (0,)), ((),...  19.8 us
    unnamed x22, local copies, waits for them, and re-layouts  18.6 us
    all_to_all x1, waiting for transfers between devices, shards(): lax.all_to_all(query_rows, 'seq', split_axis=2, concat_axis=1, tiled=True)  13.4 us
    all_to_all x1, waiting for transfers between devices, shards(): lax.all_to_all(key_rows, 'seq', split_axis=2, concat_axis=1, tiled=True)  13.3 us
    all_to_all x1, waiting for transfers between devices, shards(): lax.all_to_all(grad_query_pos, 'seq', split_axis=1, concat_axis=2, tiled=...  12 us
    dot_general x1, matrix products, attend_back(): jnp.einsum('fphd,tphd->phft', cot_heads, value_heads, preferred_element_t...  9.03 us
  transfers between devices with their start and end apart: 8, of which 5 were waited for; matrix products, arithmetic and copies ran while one was open for 35% of the time, Pallas kernels for 0%

profile of v1, /device:TPU:0, one launch (start us, length us, event | category | flops | bytes accessed | tf_op | source)
XLA Modules:
  0.0 281.2 jit_solution(15724698330337288817)
XLA Ops:
  7.2 0.0 copy-start
  7.2 3.6 %copy.96 = bf16[2,1,256,1152]{3,0,1,2:T(2,128)(2,1)} copy(bf16[2,1,256,1152]{3,2,1,0:T(8,128)(2,1)} %param.7) | data formatting | bytes 2359296 | tf_op args[0]
  10.8 5.2 %all-to-all-start = ((bf16[2,1,256,1152]{3,0,1,2:T(2,128)(2,1)}), bf16[2,1,256,1152]{3,0,1,2:T(2,128)(2,1)}, u32[]{:S(2)}, u32[]{:S(2)}) async-start(bf16[2,1,256,1152]{3,0,1,2:T(2,128)(2,1)} %copy.96), calls=%async_computation | async-start | bytes 2359296 | tf_op jit(solution)/shard_map/all_to_all | solution.py:85
  16.0 3.5 %copy.98 = bf16[2,1,256,1152]{3,0,1,2:T(2,128)(2,1)} copy(bf16[2,1,256,1152]{3,2,1,0:T(8,128)(2,1)} %param.8) | data formatting | bytes 2359296 | tf_op args[1]
  19.5 13.4 %all-to-all-done = bf16[2,1,256,1152]{3,0,1,2:T(2,128)(2,1)} async-done(((bf16[2,1,256,1152]{3,0,1,2:T(2,128)(2,1)}), bf16[2,1,256,1152]{3,0,1,2:T(2,128)(2,1)}, u32[]{:S(2)}, u32[]{:S(2)}) %all-to-all-start) | async-done | bytes 1179680 | tf_op jit(solution)/shard_map/all_to_all | solution.py:85
  32.9 4.3 %all-to-all-start.1 = ((bf16[2,1,256,1152]{3,0,1,2:T(2,128)(2,1)}), bf16[2,1,256,1152]{3,0,1,2:T(2,128)(2,1)}, u32[]{:S(2)}, u32[]{:S(2)}) async-start(bf16[2,1,256,1152]{3,0,1,2:T(2,128)(2,1)} %copy.98), calls=%async_computation.1 | async-start | bytes 2359296 | tf_op jit(solution)/shard_map/all_to_all | solution.py:86
  37.2 0.0 copy-start.6
  37.2 0.0 copy-start.5
  37.2 3.5 %copy.102 = bf16[2,1,256,1152]{3,0,1,2:T(2,128)(2,1)} copy(bf16[2,1,256,1152]{3,2,1,0:T(8,128)(2,1)} %param.9) | data formatting | bytes 2359296 | tf_op args[2]
  40.7 13.3 %all-to-all-done.1 = bf16[2,1,256,1152]{3,0,1,2:T(2,128)(2,1)} async-done(((bf16[2,1,256,1152]{3,0,1,2:T(2,128)(2,1)}), bf16[2,1,256,1152]{3,0,1,2:T(2,128)(2,1)}, u32[]{:S(2)}, u32[]{:S(2)}) %all-to-all-start.1) | async-done | bytes 1179680 | tf_op jit(solution)/shard_map/all_to_all | solution.py:86
  54.0 4.3 %all-to-all-start.2 = ((bf16[2,1,256,1152]{3,0,1,2:T(2,128)(2,1)}), bf16[2,1,256,1152]{3,0,1,2:T(2,128)(2,1)}, u32[]{:S(2)}, u32[]{:S(2)}) async-start(bf16[2,1,256,1152]{3,0,1,2:T(2,128)(2,1)} %copy.102), calls=%async_computation.2 | async-start | bytes 2359296 | tf_op jit(solution)/shard_map/all_to_all | solution.py:87
  58.3 0.6 reduce-scatter.4.cloned.1.call-start
  58.8 0.0 copy-done.6
  58.8 0.1 broadcast_compare_fusion
  58.9 0.0 copy-done.5
  58.9 0.1 iota_compare_fusion
  59.0 0.1 broadcast_and_fusion
  59.1 6.5 %reshape.215 = bf16[2,8,32,16,72]{4,3,0,2,1:T(8,128)(2,1)} reshape(bf16[2,1,256,1152]{3,0,1,2:T(2,128)(2,1)} %all-to-all-done) | data formatting | bytes 2359296 | tf_op jit(solution)/shard_map/vmap()/reshape | solution.py:19
  65.6 6.5 %reshape.216 = bf16[2,8,32,16,72]{4,3,0,2,1:T(8,128)(2,1)} reshape(bf16[2,1,256,1152]{3,0,1,2:T(2,128)(2,1)} %all-to-all-done.1) | data formatting | bytes 2359296 | tf_op jit(solution)/shard_map/vmap()/reshape | solution.py:20
  72.1 8.7 %fusion.38 = (f32[2,32,16,8]{3,2,1,0:T(8,128)S(1)}, f32[2,32,16,8,8]{3,4,2,1,0:T(8,128)}) fusion(f32[2,8]{1,0:T(2,128)S(1)} %get-tuple-element.31, pred[2,8]{1,0:T(4,128)(4,1)S(1)} %get-tuple-element.30, bf16[2,8,32,16,72]{4,3,0,2,1:T(8,128)(2,1)} %reshape.216, bf16[2,8,32,16,72]{4,3,0,2,1:T(8,128)(2,1)} %reshape.215), kind=kOutput, calls=%fused_computation.48 | convolution fusion | flops 9764871 | bytes 2654288 | tf_op jit(solution)/shard_map/vmap()/sub | solution.py:28
  80.8 0.0 all-to-all-done.2
  80.9 6.5 %reshape.217 = bf16[2,8,32,16,72]{4,3,0,2,1:T(8,128)(2,1)} reshape(bf16[2,1,256,1152]{3,0,1,2:T(2,128)(2,1)} %all-to-all-done.2) | data formatting | bytes 2359296 | tf_op jit(solution)/shard_map/vmap()/reshape | solution.py:21
  87.4 4.1 %convolution_bitcast_fusion.1 = bf16[2,8,32,16,72]{4,1,3,2,0:T(8,128)(2,1)S(1)} fusion(bf16[2,8,32,16,72]{4,3,0,2,1:T(8,128)(2,1)} %reshape.217, f32[2,32,16,8,8]{3,4,2,1,0:T(8,128)} %get-tuple-element.33, f32[2,32,16,8]{3,2,1,0:T(8,128)S(1)} %get-tuple-element.32), kind=kOutput, calls=%fused_computation.13 | convolution fusion | flops 9568256 | bytes 2654208 | tf_op jit(solution)/shard_map/vmap(phft,tphd->fphd)/dot_general | solution.py:31
  91.4 1.7 copy.106
  93.2 4.6 %reshape.203 = bf16[2,8,32,1152]{3,2,1,0:T(8,128)(2,1)} reshape(bf16[2,8,32,16,72]{4,3,2,1,0:T(8,128)(2,1)} %copy.106) | data formatting | bytes 2359296 | tf_op jit(solution)/shard_map/vmap()/reshape | solution.py:32
  97.7 1.5 select_convert_fusion
  99.3 0.1 copy.107
  99.4 0.0 copy-start.4
  99.4 20.7 %all_to_all.81 = bf16[2,8,32,1152]{3,2,0,1:T(8,128)(2,1)S(1)} all-to-all(bf16[2,8,32,1152]{3,2,0,1:T(8,128)(2,1)S(1)} %copy.107), channel_id=1, replica_groups=mesh['seq'=8,'rep'=4] {'seq'}, dimensions={1} | all-to-all | bytes 2359296 | tf_op jit(solution)/shard_map/all_to_all | solution.py:98
  120.2 0.1 copy.108
  120.3 0.0 copy-start.1
  120.3 1.0 copy-done.1
  121.3 4.1 %convolution_bitcast_fusion = f32[1152,1152]{0,1:T(8,128)} fusion(bf16[512,1152]{1,0:T(8,128)(2,1)S(1)} %bitcast.60, bf16[512,1152]{1,0:T(8,128)(2,1)S(1)} %bitcast.66), kind=kOutput, calls=%fused_computation.1 | convolution fusion | flops 1358954496 | bytes 7667712 | tf_op jit(solution)/shard_map/dot_general | solution.py:71
  125.4 6.9 %copy.136 = f32[1152,1152]{1,0:T(8,128)} copy(f32[1152,1152]{0,1:T(8,128)} %convolution_bitcast_fusion) | data formatting | bytes 10616832
  132.3 0.0 reduce-scatter.4.cloned.1.call-update
  132.3 0.1 compare_and_fusion
  132.4 3.1 %fusion.3 = bf16[2,1,256,1152]{3,2,0,1:T(8,128)(2,1)S(1)} fusion(bf16[1152,1152]{1,0:T(8,128)(2,1)S(1)} %copy-done, bf16[2,1,256,1152]{3,2,1,0:T(8,128)(2,1)} %param.10, pred[2,256]{1,0:T(4,128)(4,1)S(1)} %compare_and_fusion), kind=kOutput, calls=%fused_computation.10 | convolution fusion | flops 1360134144 | bytes 5014016 | tf_op jit(solution)/shard_map/dot_general | solution.py:108
  135.5 1.2 copy.109
  136.7 19.9 %all_to_all.82 = bf16[2,1,256,1152]{3,0,1,2:T(2,128)(2,1)} all-to-all(bf16[2,1,256,1152]{3,0,1,2:T(2,128)(2,1)S(1)} %copy.109), channel_id=1, replica_groups=mesh['seq'=8,'rep'=4] {'seq'}, dimensions={2} | all-to-all | bytes 2359296 | tf_op jit(solution)/shard_map/all_to_all | solution.py:112
  156.6 6.5 %reshape.218 = bf16[2,8,32,16,72]{4,3,0,2,1:T(8,128)(2,1)} reshape(bf16[2,1,256,1152]{3,0,1,2:T(2,128)(2,1)} %all_to_all.82) | data formatting | bytes 2359296 | tf_op jit(solution)/shard_map/vmap()/reshape | solution.py:43
  163.1 4.7 %convert_bitcast_fusion = bf16[2,8,32,16,72]{4,1,3,2,0:T(8,128)(2,1)S(1)} fusion(bf16[2,8,32,16,72]{4,3,0,2,1:T(8,128)(2,1)} %reshape.218, f32[2,32,16,8,8]{3,4,2,1,0:T(8,128)} %get-tuple-element.33, f32[2,32,16,8]{3,2,1,0:T(8,128)S(1)} %get-tuple-element.32), kind=kOutput, calls=%fused_computation.14 | convolution fusion | flops 10158080 | bytes 2654208 | tf_op jit(solution)/shard_map/vmap(phft,fphd->tphd)/dot_general | solution.py:45
  167.9 1.8 copy.135
  169.7 4.6 %reshape.212 = bf16[2,8,32,1152]{3,2,0,1:T(8,128)(2,1)} reshape(bf16[2,8,32,16,72]{4,3,2,0,1:T(8,128)(2,1)} %copy.135) | data formatting | bytes 2359296 | tf_op jit(solution)/shard_map/vmap()/convert_element_type | solution.py:65
  174.3 4.3 %all-to-all-start.7 = ((bf16[2,8,32,1152]{3,2,0,1:T(8,128)(2,1)}), bf16[2,8,32,1152]{3,2,0,1:T(8,128)(2,1)}, u32[]{:S(2)}, u32[]{:S(2)}) async-start(bf16[2,8,32,1152]{3,2,0,1:T(8,128)(2,1)} %reshape.212), calls=%async_computation.7 | async-start | bytes 2359296 | tf_op jit(solution)/shard_map/all_to_all | solution.py:119
  178.5 0.3 all-gather.3.cloned.1.call-start
  178.8 19.8 %reduce-scatter.4.cloned.1.call-done = f32[144,1152]{1,0:T(8,128)} async-done(((f32[1152,1152]{1,0:T(8,128)}), f32[144,1152]{1,0:T(8,128)}) %reduce-scatter.4.cloned.1.call-update) | async-done | bytes 663568 | tf_op jit(solution)/shard_map/reduce_scatter | solution.py:70
  198.6 0.0 all-gather.3.cloned.1.call-update
  198.6 9.0 %multiply_reduce_fusion = (f32[2,32,16,8]{3,2,1,0:T(8,128)S(1)}, f32[2,32,16,8,8]{3,4,2,1,0:T(8,128)}) fusion(f32[2,32,16,8,8]{3,4,2,1,0:T(8,128)} %get-tuple-element.33, f32[2,32,16,8]{3,2,1,0:T(8,128)S(1)} %get-tuple-element.32, bf16[2,8,32,16,72]{4,3,0,2,1:T(8,128)(2,1)} %reshape.217, bf16[2,8,32,16,72]{4,3,0,2,1:T(8,128)(2,1)} %reshape.218), kind=kOutput, calls=%fused_computation.3 | convolution fusion | flops 9625600 | bytes 2949120 | tf_op jit(solution)/shard_map/vmap(fphd,tphd->phft)/dot_general | solution.py:48
  207.7 7.6 %convert_bitcast_fusion.1 = bf16[2,8,32,16,72]{4,1,3,2,0:T(8,128)(2,1)S(1)} fusion(bf16[2,8,32,16,72]{4,3,0,2,1:T(8,128)(2,1)S(1)} %copy-done.3, f32[2,32,16,8,8]{3,4,2,1,0:T(8,128)} %get-tuple-element.35, f32[2,32,16,8]{3,2,1,0:T(8,128)S(1)} %get-tuple-element.34, f32[2,32,16,8,8]{3,4,2,1,0:T(8,128)S(1)} %copy-done.7, ...), kind=kOutput, calls=%fused_computation.15 | convolution fusion | flops 57475072 | bytes 2949120 | tf_op jit(solution)/shard_map/vmap(phft,fphd->tphd)/dot_general | solution.py:58
  215.3 1.8 copy.134
  217.1 4.6 %reshape.211 = bf16[2,8,32,1152]{3,2,0,1:T(8,128)(2,1)} reshape(bf16[2,8,32,16,72]{4,3,2,0,1:T(8,128)(2,1)} %copy.134) | data formatting | bytes 2359296 | tf_op jit(solution)/shard_map/vmap()/convert_element_type | solution.py:64
  221.7 0.0 all-to-all-done.7
  221.7 6.3 %all-to-all-start.6 = ((bf16[2,8,32,1152]{3,2,0,1:T(8,128)(2,1)}), bf16[2,8,32,1152]{3,2,0,1:T(8,128)(2,1)}, u32[]{:S(2)}, u32[]{:S(2)}) async-start(bf16[2,8,32,1152]{3,2,0,1:T(8,128)(2,1)} %reshape.211), calls=%async_computation.6 | async-start | bytes 2359296 | tf_op jit(solution)/shard_map/all_to_all | solution.py:118
  228.0 8.3 %convert_bitcast_fusion.2 = bf16[2,8,32,16,72]{4,1,3,2,0:T(8,128)(2,1)S(1)} fusion(bf16[2,8,32,16,72]{4,3,0,2,1:T(8,128)(2,1)} %reshape.216, f32[2,32,16,8,8]{3,4,2,1,0:T(8,128)} %get-tuple-element.35, f32[2,32,16,8]{3,2,1,0:T(8,128)} %copy-done.8, f32[2,32,16,8,8]{3,4,2,1,0:T(8,128)} %get-tuple-element.33, f32[2,32,16,8]{3,2,1,0:T(8,128)S(1)} %get-tuple-element.32), kind=kOutput, calls=%fused_computation.16 | convolution fusion | flops 57475072 | bytes 2949120 | tf_op jit(solution)/shard_map/vmap(phft,tphd->fphd)/dot_general | solution.py:55
  236.3 1.8 copy.133
  238.0 4.6 %reshape.210 = bf16[2,8,32,1152]{3,2,0,1:T(8,128)(2,1)} reshape(bf16[2,8,32,16,72]{4,3,2,0,1:T(8,128)(2,1)} %copy.133) | data formatting | bytes 2359296 | tf_op jit(solution)/shard_map/vmap()/convert_element_type | solution.py:63
  242.6 2.2 all-to-all-done.6
  244.8 4.3 %all-to-all-start.5 = ((bf16[2,8,32,1152]{3,2,0,1:T(8,128)(2,1)}), bf16[2,8,32,1152]{3,2,0,1:T(8,128)(2,1)}, u32[]{:S(2)}, u32[]{:S(2)}) async-start(bf16[2,8,32,1152]{3,2,0,1:T(8,128)(2,1)} %reshape.210), calls=%async_computation.5 | async-start | bytes 2359296 | tf_op jit(solution)/shard_map/all_to_all | solution.py:117
  249.1 2.4 copy.125
  251.5 2.4 copy.121
  253.9 12.0 %all-to-all-done.5 = bf16[2,8,32,1152]{3,2,0,1:T(8,128)(2,1)} async-done(((bf16[2,8,32,1152]{3,2,0,1:T(8,128)(2,1)}), bf16[2,8,32,1152]{3,2,0,1:T(8,128)(2,1)}, u32[]{:S(2)}, u32[]{:S(2)}) %all-to-all-start.5) | async-done | bytes 1179680 | tf_op jit(solution)/shard_map/all_to_all | solution.py:117
  265.9 2.5 copy.117
  268.4 2.9 %convolution_convert_fusion = bf16[512,1152]{1,0:T(8,128)(2,1)} fusion(bf16[512,1152]{1,0:T(8,128)(2,1)S(1)} %bitcast.61, bf16[1152,1152]{1,0:T(8,128)(2,1)S(1)} %copy-done), kind=kOutput, calls=%fused_computation.8 | convolution fusion | flops 1359544320 | bytes 5013504 | tf_op jit(solution)/shard_map/dot_general | solution.py:101
  271.3 2.8 reduce_sum.29
  (13 shorter events, 0.0 us)
Async XLA Ops:
  7.2 125.2 %copy-start = (bf16[1152,1152]{1,0:T(8,128)(2,1)S(1)}, bf16[1152,1152]{1,0:T(8,128)(2,1)}, u32[]{:S(2)}) copy-start(bf16[1152,1152]{1,0:T(8,128)(2,1)} %param.11) | copy-start | bytes 7962628
  10.8 22.1 %all-to-all-start = ((bf16[2,1,256,1152]{3,0,1,2:T(2,128)(2,1)}), bf16[2,1,256,1152]{3,0,1,2:T(2,128)(2,1)}, u32[]{:S(2)}, u32[]{:S(2)}) async-start(bf16[2,1,256,1152]{3,0,1,2:T(2,128)(2,1)} %copy.96), calls=%async_computation | async-start | bytes 2359296 | tf_op jit(solution)/shard_map/all_to_all | solution.py:85
  32.9 21.1 %all-to-all-start.1 = ((bf16[2,1,256,1152]{3,0,1,2:T(2,128)(2,1)}), bf16[2,1,256,1152]{3,0,1,2:T(2,128)(2,1)}, u32[]{:S(2)}, u32[]{:S(2)}) async-start(bf16[2,1,256,1152]{3,0,1,2:T(2,128)(2,1)} %copy.98), calls=%async_computation.1 | async-start | bytes 2359296 | tf_op jit(solution)/shard_map/all_to_all | solution.py:86
  37.2 21.6 %copy-start.6 = (s32[2]{0:T(128)S(1)}, s32[2]{0:T(128)}, u32[]{:S(2)}) copy-start(s32[2]{0:T(128)} %param.13) | copy-start | bytes 28
  37.2 21.7 %copy-start.5 = (s32[2]{0:T(128)S(1)}, s32[2]{0:T(128)}, u32[]{:S(2)}) copy-start(s32[2]{0:T(128)} %param.12) | copy-start | bytes 28
  54.0 26.9 %all-to-all-start.2 = ((bf16[2,1,256,1152]{3,0,1,2:T(2,128)(2,1)}), bf16[2,1,256,1152]{3,0,1,2:T(2,128)(2,1)}, u32[]{:S(2)}, u32[]{:S(2)}) async-start(bf16[2,1,256,1152]{3,0,1,2:T(2,128)(2,1)} %copy.102), calls=%async_computation.2 | async-start | bytes 2359296 | tf_op jit(solution)/shard_map/all_to_all | solution.py:87
  58.3 140.3 %reduce-scatter.4.cloned.1.call-start = ((), (), s32[]{:S(2)}) async-start(), calls=%async_computation.10 | async-start | bytes 5971968 | tf_op jit(solution)/shard_map/reduce_scatter | solution.py:70
  99.4 21.9 %copy-start.4 = (bf16[2,1,256,1152]{3,2,1,0:T(8,128)(2,1)S(1)}, bf16[2,1,256,1152]{3,2,1,0:T(8,128)(2,1)}, u32[]{:S(2)}) copy-start(bf16[2,1,256,1152]{3,2,1,0:T(8,128)(2,1)} %param.10) | copy-start | bytes 3538948
  120.3 1.0 copy-start.1
  174.3 47.4 %all-to-all-start.7 = ((bf16[2,8,32,1152]{3,2,0,1:T(8,128)(2,1)}), bf16[2,8,32,1152]{3,2,0,1:T(8,128)(2,1)}, u32[]{:S(2)}, u32[]{:S(2)}) async-start(bf16[2,8,32,1152]{3,2,0,1:T(8,128)(2,1)} %reshape.212), calls=%async_computation.7 | async-start | bytes 2359296 | tf_op jit(solution)/shard_map/all_to_all | solution.py:119
  178.5 92.8 %all-gather.3.cloned.1.call-start = ((), (), s32[]{:S(2)}) async-start(), calls=%async_computation.9 | async-start | bytes 3317760 | tf_op jit(solution)/shard_map/all_gather | solution.py:11
  198.6 9.1 %copy-start.3 = (bf16[2,8,32,16,72]{4,3,0,2,1:T(8,128)(2,1)S(1)}, bf16[2,8,32,16,72]{4,3,0,2,1:T(8,128)(2,1)}, u32[]{:S(2)}) copy-start(bf16[2,8,32,16,72]{4,3,0,2,1:T(8,128)(2,1)} %reshape.215) | copy-start | bytes 3538948
  198.6 9.0 %copy-start.7 = (f32[2,32,16,8,8]{3,4,2,1,0:T(8,128)S(1)}, f32[2,32,16,8,8]{3,4,2,1,0:T(8,128)}, u32[]{:S(2)}) copy-start(f32[2,32,16,8,8]{3,4,2,1,0:T(8,128)} %get-tuple-element.33) | copy-start | bytes 786436
  207.7 7.6 %copy-start.8 = (f32[2,32,16,8]{3,2,1,0:T(8,128)}, f32[2,32,16,8]{3,2,1,0:T(8,128)S(1)}, u32[]{:S(2)}) copy-start(f32[2,32,16,8]{3,2,1,0:T(8,128)S(1)} %get-tuple-element.34) | copy-start | bytes 98308
  221.7 23.1 %all-to-all-start.6 = ((bf16[2,8,32,1152]{3,2,0,1:T(8,128)(2,1)}), bf16[2,8,32,1152]{3,2,0,1:T(8,128)(2,1)}, u32[]{:S(2)}, u32[]{:S(2)}) async-start(bf16[2,8,32,1152]{3,2,0,1:T(8,128)(2,1)} %reshape.211), calls=%async_computation.6 | async-start | bytes 2359296 | tf_op jit(solution)/shard_map/all_to_all | solution.py:118
  244.8 21.1 %all-to-all-start.5 = ((bf16[2,8,32,1152]{3,2,0,1:T(8,128)(2,1)}), bf16[2,8,32,1152]{3,2,0,1:T(8,128)(2,1)}, u32[]{:S(2)}, u32[]{:S(2)}) async-start(bf16[2,8,32,1152]{3,2,0,1:T(8,128)(2,1)} %reshape.210), calls=%async_computation.5 | async-start | bytes 2359296 | tf_op jit(solution)/shard_map/all_to_all | solution.py:117
  265.9 2.5 copy-start.2
Sparse Core Ops, SparseCore 0:
  132.4 66.1 reduce-scatter.3
  200.1 57.8 all-gather.2
